TPU v7x, 32 devices: a whole 2x2x4 slice. The times are simulated.
32 devices in a mesh: groups: 2 (over x), ctx: 16 (over z, y, core).
Axes of the slice: x: 2, y: 2, z: 4, core: 2. Of those that a mesh axis runs over, the one named last changes fastest.
Arguments:
- queries: bfloat16 [8192, 1024], P(('groups', 'ctx')), parts along dimension 0, may hold values from -7 to 7
- keys: bfloat16 [8192, 128], P(('groups', 'ctx')), parts along dimension 0, may hold values from -7 to 7
- values: bfloat16 [8192, 128], P(('groups', 'ctx')), parts along dimension 0, may hold values from -6 to 6
- span_order: int32 [64], P('groups'), parts along dimension 0, may hold values from 0 to 31, as said below
Outputs:
- attended: bfloat16 [8192, 1024], P(('groups', 'ctx')), parts along dimension 0
There are 2 independent parts, one for each index of `groups`. A program takes and returns all parts, laid end to end along the dimension named above; each array names one. Nothing has to cross between parts.
Inputs may be any that keep to these rules, and one draw needn't show every extreme that they name: A permutation: rows j * 128 to (j + 1) * 128 - 1 hold span span_order[j] of the sequence; for every j, span_order[2 j] + span_order[2 j + 1] = 31.
All inputs are finite; a program needn't handle non-finite values.
Results may differ from a plain program's by a relative error of at most 0.006.
Values may be sent and summed in bfloat16 or wider, within the bound.
A program may use at most 64 MiB of HBM per device.

v0:
```python
import math

import jax
import jax.numpy as jnp
from jax import lax
from jax.sharding import PartitionSpec as P


def body(queries, keys, values, span_order):
    local_rows = queries.shape[0]
    head_size = keys.shape[1]
    heads = queries.shape[1] // head_size
    span = local_rows // 2
    device = lax.axis_index("ctx")
    key_positions = (
        span_order[:, None] * span + jnp.arange(span, dtype=jnp.int32)[None, :]
    ).reshape(-1)
    query_pos = lax.dynamic_slice_in_dim(key_positions, device * local_rows, local_rows, 0)
    query_heads = queries.reshape(local_rows, heads, head_size)
    scale = 1.0 / math.sqrt(head_size)

    def update(carry, key_blk, value_blk, key_pos):
        running, total, accum = carry
        score = (
            jnp.einsum("qhd,kd->hqk", query_heads, key_blk, preferred_element_type=jnp.float32)
            * scale
        )
        kept = key_pos[None, None, :] <= query_pos[None, :, None]
        score = jnp.where(kept, score, jnp.float32(-1e30))
        fresh = jnp.maximum(running, jnp.max(score, axis=-1))
        factor = jnp.exp(running - fresh)
        weight = jnp.where(kept, jnp.exp(score - fresh[:, :, None]), jnp.float32(0.0))
        total = total * factor + jnp.sum(weight, axis=-1)
        accum = accum * factor[:, :, None] + jnp.einsum(
            "hqk,kd->hqd",
            weight.astype(jnp.bfloat16),
            value_blk,
            preferred_element_type=jnp.float32,
        )
        return (fresh, total, accum)

    initial = (
        jnp.full((heads, local_rows), -1e30, jnp.float32),
        jnp.zeros((heads, local_rows), jnp.float32),
        jnp.zeros((heads, local_rows, head_size), jnp.float32),
    )
    key_piece = lax.all_gather(keys, "ctx", axis=0, tiled=True)
    value_piece = lax.all_gather(values, "ctx", axis=0, tiled=True)
    count = key_piece.shape[0]
    block = math.gcd(count, 512)

    def step(index, state):
        first = (index * block).astype(jnp.int32)
        key_blk = lax.dynamic_slice_in_dim(key_piece, first, block, 0)
        value_blk = lax.dynamic_slice_in_dim(value_piece, first, block, 0)
        key_pos = lax.dynamic_slice_in_dim(key_positions, first, block, 0)
        return update(state, key_blk, value_blk, key_pos)

    running, total, accum = lax.fori_loop(0, count // block, step, initial)
    mixed = accum / total[:, :, None]
    return (
        jnp.transpose(mixed, (1, 0, 2)).reshape(local_rows, heads * head_size).astype(jnp.bfloat16)
    )


def solution(mesh):
    in_specs = (
        P(("groups", "ctx"), None),
        P(("groups", "ctx"), None),
        P(("groups", "ctx"), None),
        P("groups"),
    )
    out_specs = P(("groups", "ctx"), None)
    return jax.shard_map(body, mesh=mesh, in_specs=in_specs, out_specs=out_specs, check_vma=False)
```

profile of v0, /device:TPU:1, one launch (start us, length us, event | category | flops | bytes accessed | tf_op | source)
XLA Modules:
  0.0 141.4 jit_solution(1959519106321978832)
XLA Ops:
  6.5 0.0 all-gather.3.cloned.1.call-start
  6.5 0.7 all-gather.3.cloned.1.call-update
  7.3 0.0 all-gather.5.cloned.1.call-start
  7.3 0.7 all-gather.5.cloned.1.call-update
  8.0 1.2 copy.8
  9.3 0.3 copy.9
  9.6 0.7 broadcast_multiply_fusion
  10.2 0.1 add_bitcast_fusion
  10.3 0.1 dynamic_slice.24
  10.4 39.5 %all-gather.3.cloned.1.call-done = bf16[4096,128]{1,0:T(8,128)(2,1)} async-done(((bf16[256,128]{1,0:T(8,128)(2,1)}), bf16[4096,128]{1,0:T(8,128)(2,1)}) %all-gather.3.cloned.1.call-update) | async-done | bytes 1048592 | tf_op jit(solution)/shard_map/all_gather | solution.py:47
  49.8 39.0 %all-gather.5.cloned.1.call-done = bf16[4096,128]{1,0:T(8,128)(2,1)} async-done(((bf16[256,128]{1,0:T(8,128)(2,1)}), bf16[4096,128]{1,0:T(8,128)(2,1)}) %all-gather.5.cloned.1.call-update) | async-done | bytes 1048592 | tf_op jit(solution)/shard_map/all_gather | solution.py:48
  88.9 44.5 %while.18 = (s32[]{:T(128)}, f32[8,256]{1,0:T(8,128)S(1)}, f32[8,256]{1,0:T(8,128)S(1)}, f32[8,256,128]{2,1,0:T(8,128)S(1)}, s32[4096]{0:T(1024)S(1)}, /*index=5...) while((s32[]{:T(128)}, f32[8,256]{1,0:T(8,128)S(1)}, ...), condition=%wide.region_3.4_spmd.clone, body=%wide.region_0.3_spmd.clone.sunk | while | flops 551430144 | bytes 16129227 | solution.py:59
  88.9 0.1 dynamic_slice.43
  88.9 0.1 broadcast_compare_fusion.2
  89.1 1.7 %fusion.33 = (f32[8,256]{1,0:T(8,128)S(1)}, f32[512,256,8]{1,0,2:T(8,128)S(1)}) fusion(pred[256,512]{0,1:T(8,128)(4,1)S(1)} %broadcast_compare_fusion.2, bf16[256,8,128]{2,0,1:T(8,128)(2,1)S(1)} %get-tuple-element.319, bf16[4096,128]{1,0:T(8,128)(2,1)} %get-tuple-element.318, s32[]{:T(128)S(6)} %select_n.62), kind=kOutput, calls=%fused_computation.2.clone.1 | convolution fusion | flops 271579136 | bytes 4988932 | tf_op jit(solution)/shard_map/while/body/eval_jaxpr/qhd,kd->hqk/dot_general | solution.py:25
  90.8 1.0 fusion.34
  91.8 2.6 %fusion.36 = f32[8,256,128]{2,1,0:T(8,128)S(1)} fusion(f32[512,256,8]{1,0,2:T(8,128)S(1)} %get-tuple-element.283, f32[8,256]{1,0:T(8,128)S(1)} %select_maximum_fusion.2, pred[256,512]{0,1:T(8,128)(4,1)S(1)} %broadcast_compare_fusion.2, f32[8,256,128]{2,1,0:T(8,128)S(1)} %get-tuple-element.302, f32[8,256]{1,0:T(8,128)S(1)} %get-tuple-element.285, ...), kind=kOutput, calls=%fused_computation.7.clone.1 | convolution fusion | flops 274464768 | bytes 6569989 | tf_op jit(solution)/shard_map/while/body/eval_jaxpr/hqk,kd->hqd/dot_general | solution.py:34
  94.4 0.1 dynamic_slice.43
  94.5 0.1 broadcast_compare_fusion.2
  94.7 1.7 %fusion.33 = (f32[8,256]{1,0:T(8,128)S(1)}, f32[512,256,8]{1,0,2:T(8,128)S(1)}) fusion(pred[256,512]{0,1:T(8,128)(4,1)S(1)} %broadcast_compare_fusion.2, bf16[256,8,128]{2,0,1:T(8,128)(2,1)S(1)} %get-tuple-element.319, bf16[4096,128]{1,0:T(8,128)(2,1)} %get-tuple-element.318, s32[]{:T(128)S(6)} %select_n.62), kind=kOutput, calls=%fused_computation.2.clone.1 | convolution fusion | flops 271579136 | bytes 4988932 | tf_op jit(solution)/shard_map/while/body/eval_jaxpr/qhd,kd->hqk/dot_general | solution.py:25
  96.4 1.0 fusion.34
  97.4 2.6 %fusion.36 = f32[8,256,128]{2,1,0:T(8,128)S(1)} fusion(f32[512,256,8]{1,0,2:T(8,128)S(1)} %get-tuple-element.283, f32[8,256]{1,0:T(8,128)S(1)} %select_maximum_fusion.2, pred[256,512]{0,1:T(8,128)(4,1)S(1)} %broadcast_compare_fusion.2, f32[8,256,128]{2,1,0:T(8,128)S(1)} %get-tuple-element.302, f32[8,256]{1,0:T(8,128)S(1)} %get-tuple-element.285, ...), kind=kOutput, calls=%fused_computation.7.clone.1 | convolution fusion | flops 274464768 | bytes 6569989 | tf_op jit(solution)/shard_map/while/body/eval_jaxpr/hqk,kd->hqd/dot_general | solution.py:34
  100.0 0.1 dynamic_slice.43
  100.1 0.1 broadcast_compare_fusion.2
  100.2 1.7 %fusion.33 = (f32[8,256]{1,0:T(8,128)S(1)}, f32[512,256,8]{1,0,2:T(8,128)S(1)}) fusion(pred[256,512]{0,1:T(8,128)(4,1)S(1)} %broadcast_compare_fusion.2, bf16[256,8,128]{2,0,1:T(8,128)(2,1)S(1)} %get-tuple-element.319, bf16[4096,128]{1,0:T(8,128)(2,1)} %get-tuple-element.318, s32[]{:T(128)S(6)} %select_n.62), kind=kOutput, calls=%fused_computation.2.clone.1 | convolution fusion | flops 271579136 | bytes 4988932 | tf_op jit(solution)/shard_map/while/body/eval_jaxpr/qhd,kd->hqk/dot_general | solution.py:25
  101.9 1.0 fusion.34
  103.0 2.6 %fusion.36 = f32[8,256,128]{2,1,0:T(8,128)S(1)} fusion(f32[512,256,8]{1,0,2:T(8,128)S(1)} %get-tuple-element.283, f32[8,256]{1,0:T(8,128)S(1)} %select_maximum_fusion.2, pred[256,512]{0,1:T(8,128)(4,1)S(1)} %broadcast_compare_fusion.2, f32[8,256,128]{2,1,0:T(8,128)S(1)} %get-tuple-element.302, f32[8,256]{1,0:T(8,128)S(1)} %get-tuple-element.285, ...), kind=kOutput, calls=%fused_computation.7.clone.1 | convolution fusion | flops 274464768 | bytes 6569989 | tf_op jit(solution)/shard_map/while/body/eval_jaxpr/hqk,kd->hqd/dot_general | solution.py:34
  105.6 0.1 dynamic_slice.43
  105.6 0.1 broadcast_compare_fusion.2
  105.8 1.7 %fusion.33 = (f32[8,256]{1,0:T(8,128)S(1)}, f32[512,256,8]{1,0,2:T(8,128)S(1)}) fusion(pred[256,512]{0,1:T(8,128)(4,1)S(1)} %broadcast_compare_fusion.2, bf16[256,8,128]{2,0,1:T(8,128)(2,1)S(1)} %get-tuple-element.319, bf16[4096,128]{1,0:T(8,128)(2,1)} %get-tuple-element.318, s32[]{:T(128)S(6)} %select_n.62), kind=kOutput, calls=%fused_computation.2.clone.1 | convolution fusion | flops 271579136 | bytes 4988932 | tf_op jit(solution)/shard_map/while/body/eval_jaxpr/qhd,kd->hqk/dot_general | solution.py:25
  107.5 1.0 fusion.34
  108.5 2.6 %fusion.36 = f32[8,256,128]{2,1,0:T(8,128)S(1)} fusion(f32[512,256,8]{1,0,2:T(8,128)S(1)} %get-tuple-element.283, f32[8,256]{1,0:T(8,128)S(1)} %select_maximum_fusion.2, pred[256,512]{0,1:T(8,128)(4,1)S(1)} %broadcast_compare_fusion.2, f32[8,256,128]{2,1,0:T(8,128)S(1)} %get-tuple-element.302, f32[8,256]{1,0:T(8,128)S(1)} %get-tuple-element.285, ...), kind=kOutput, calls=%fused_computation.7.clone.1 | convolution fusion | flops 274464768 | bytes 6569989 | tf_op jit(solution)/shard_map/while/body/eval_jaxpr/hqk,kd->hqd/dot_general | solution.py:34
  111.1 0.1 dynamic_slice.43
  111.2 0.1 broadcast_compare_fusion.2
  111.4 1.7 %fusion.33 = (f32[8,256]{1,0:T(8,128)S(1)}, f32[512,256,8]{1,0,2:T(8,128)S(1)}) fusion(pred[256,512]{0,1:T(8,128)(4,1)S(1)} %broadcast_compare_fusion.2, bf16[256,8,128]{2,0,1:T(8,128)(2,1)S(1)} %get-tuple-element.319, bf16[4096,128]{1,0:T(8,128)(2,1)} %get-tuple-element.318, s32[]{:T(128)S(6)} %select_n.62), kind=kOutput, calls=%fused_computation.2.clone.1 | convolution fusion | flops 271579136 | bytes 4988932 | tf_op jit(solution)/shard_map/while/body/eval_jaxpr/qhd,kd->hqk/dot_general | solution.py:25
  113.1 1.0 fusion.34
  114.1 2.6 %fusion.36 = f32[8,256,128]{2,1,0:T(8,128)S(1)} fusion(f32[512,256,8]{1,0,2:T(8,128)S(1)} %get-tuple-element.283, f32[8,256]{1,0:T(8,128)S(1)} %select_maximum_fusion.2, pred[256,512]{0,1:T(8,128)(4,1)S(1)} %broadcast_compare_fusion.2, f32[8,256,128]{2,1,0:T(8,128)S(1)} %get-tuple-element.302, f32[8,256]{1,0:T(8,128)S(1)} %get-tuple-element.285, ...), kind=kOutput, calls=%fused_computation.7.clone.1 | convolution fusion | flops 274464768 | bytes 6569989 | tf_op jit(solution)/shard_map/while/body/eval_jaxpr/hqk,kd->hqd/dot_general | solution.py:34
  116.7 0.1 dynamic_slice.43
  116.8 0.1 broadcast_compare_fusion.2
  116.9 1.7 %fusion.33 = (f32[8,256]{1,0:T(8,128)S(1)}, f32[512,256,8]{1,0,2:T(8,128)S(1)}) fusion(pred[256,512]{0,1:T(8,128)(4,1)S(1)} %broadcast_compare_fusion.2, bf16[256,8,128]{2,0,1:T(8,128)(2,1)S(1)} %get-tuple-element.319, bf16[4096,128]{1,0:T(8,128)(2,1)} %get-tuple-element.318, s32[]{:T(128)S(6)} %select_n.62), kind=kOutput, calls=%fused_computation.2.clone.1 | convolution fusion | flops 271579136 | bytes 4988932 | tf_op jit(solution)/shard_map/while/body/eval_jaxpr/qhd,kd->hqk/dot_general | solution.py:25
  118.6 1.0 fusion.34
  119.7 2.6 %fusion.36 = f32[8,256,128]{2,1,0:T(8,128)S(1)} fusion(f32[512,256,8]{1,0,2:T(8,128)S(1)} %get-tuple-element.283, f32[8,256]{1,0:T(8,128)S(1)} %select_maximum_fusion.2, pred[256,512]{0,1:T(8,128)(4,1)S(1)} %broadcast_compare_fusion.2, f32[8,256,128]{2,1,0:T(8,128)S(1)} %get-tuple-element.302, f32[8,256]{1,0:T(8,128)S(1)} %get-tuple-element.285, ...), kind=kOutput, calls=%fused_computation.7.clone.1 | convolution fusion | flops 274464768 | bytes 6569989 | tf_op jit(solution)/shard_map/while/body/eval_jaxpr/hqk,kd->hqd/dot_general | solution.py:34
  122.3 0.1 dynamic_slice.43
  122.3 0.1 broadcast_compare_fusion.2
  122.5 1.7 %fusion.33 = (f32[8,256]{1,0:T(8,128)S(1)}, f32[512,256,8]{1,0,2:T(8,128)S(1)}) fusion(pred[256,512]{0,1:T(8,128)(4,1)S(1)} %broadcast_compare_fusion.2, bf16[256,8,128]{2,0,1:T(8,128)(2,1)S(1)} %get-tuple-element.319, bf16[4096,128]{1,0:T(8,128)(2,1)} %get-tuple-element.318, s32[]{:T(128)S(6)} %select_n.62), kind=kOutput, calls=%fused_computation.2.clone.1 | convolution fusion | flops 271579136 | bytes 4988932 | tf_op jit(solution)/shard_map/while/body/eval_jaxpr/qhd,kd->hqk/dot_general | solution.py:25
  124.2 1.0 fusion.34
  125.2 2.6 %fusion.36 = f32[8,256,128]{2,1,0:T(8,128)S(1)} fusion(f32[512,256,8]{1,0,2:T(8,128)S(1)} %get-tuple-element.283, f32[8,256]{1,0:T(8,128)S(1)} %select_maximum_fusion.2, pred[256,512]{0,1:T(8,128)(4,1)S(1)} %broadcast_compare_fusion.2, f32[8,256,128]{2,1,0:T(8,128)S(1)} %get-tuple-element.302, f32[8,256]{1,0:T(8,128)S(1)} %get-tuple-element.285, ...), kind=kOutput, calls=%fused_computation.7.clone.1 | convolution fusion | flops 274464768 | bytes 6569989 | tf_op jit(solution)/shard_map/while/body/eval_jaxpr/hqk,kd->hqd/dot_general | solution.py:34
  127.8 0.1 dynamic_slice.43
  127.9 0.1 broadcast_compare_fusion.2
  128.1 1.7 %fusion.33 = (f32[8,256]{1,0:T(8,128)S(1)}, f32[512,256,8]{1,0,2:T(8,128)S(1)}) fusion(pred[256,512]{0,1:T(8,128)(4,1)S(1)} %broadcast_compare_fusion.2, bf16[256,8,128]{2,0,1:T(8,128)(2,1)S(1)} %get-tuple-element.319, bf16[4096,128]{1,0:T(8,128)(2,1)} %get-tuple-element.318, s32[]{:T(128)S(6)} %select_n.62), kind=kOutput, calls=%fused_computation.2.clone.1 | convolution fusion | flops 271579136 | bytes 4988932 | tf_op jit(solution)/shard_map/while/body/eval_jaxpr/qhd,kd->hqk/dot_general | solution.py:25
  129.8 1.0 fusion.34
  130.8 2.6 %fusion.36 = f32[8,256,128]{2,1,0:T(8,128)S(1)} fusion(f32[512,256,8]{1,0,2:T(8,128)S(1)} %get-tuple-element.283, f32[8,256]{1,0:T(8,128)S(1)} %select_maximum_fusion.2, pred[256,512]{0,1:T(8,128)(4,1)S(1)} %broadcast_compare_fusion.2, f32[8,256,128]{2,1,0:T(8,128)S(1)} %get-tuple-element.302, f32[8,256]{1,0:T(8,128)S(1)} %get-tuple-element.285, ...), kind=kOutput, calls=%fused_computation.7.clone.1 | convolution fusion | flops 274464768 | bytes 6569989 | tf_op jit(solution)/shard_map/while/body/eval_jaxpr/hqk,kd->hqd/dot_general | solution.py:34
  133.4 1.1 copy_bitcast_fusion
  (27 shorter events, 0.2 us)
Async XLA Ops:
  6.5 43.3 %all-gather.3.cloned.1.call-start = ((), (), s32[]{:S(2)}) async-start(), calls=%async_computation | async-start | bytes 1114112 | tf_op jit(solution)/shard_map/all_gather | solution.py:47
  7.3 81.6 %all-gather.5.cloned.1.call-start = ((), (), s32[]{:S(2)}) async-start(), calls=%async_computation.1 | async-start | bytes 1114112 | tf_op jit(solution)/shard_map/all_gather | solution.py:48
Sparse Core Ops, SparseCore 0:
  9.5 40.3 all-gather.2
  52.0 36.8 all-gather.4
where the time goes:
time: 142 us; the launch traced here: 141 us
  waiting for transfers between devices  79.9 us (56%)
  matrix products  33.9 us (24%)
  between operations  13.5 us (10%)
  other arithmetic  11.2 us (8%)
  local copies, waits for them, and re-layouts  2.23 us (2%)
    all_gather x1, waiting for transfers between devices, body(): key_piece = lax.all_gather(keys, 'ctx', axis=0, tiled=True)  39.5 us
    all_gather x1, waiting for transfers between devices, body(): value_piece = lax.all_gather(values, 'ctx', axis=0, tiled=True)  39 us
    dot_general x8, matrix products, update(): jnp.einsum('hqk,kd->hqd', weight.astype(jnp.bfloat16), value_blk, preferr...  20.4 us
    dot_general x8, matrix products, update(): jnp.einsum('qhd,kd->hqk', query_heads, key_blk, preferred_element_type=jn...  13.5 us
    reduce_sum x8, other arithmetic, update(): total = total * factor + jnp.sum(weight, axis=-1)  8.06 us
  transfers between devices with their start and end apart: 2, of which 2 were waited for; matrix products, arithmetic and copies ran while one was open for 2% of the time, Pallas kernels for 0%

commit v1 on v0

v1 whole, which is shorter than its diff:
```python
import functools
import math

import jax
import jax.numpy as jnp
from jax import lax
from jax.experimental import pallas as pl
from jax.experimental.pallas import tpu as pltpu
from jax.sharding import PartitionSpec as P

UP, DOWN, SIDE, TWIN = 0, 1, 2, 3
NEG = -1e30


def gather_kernel(n, k_ref, v_ref, buf, send_sem, recv_sem):
    lanes = 4
    zs = n // lanes
    me = lax.axis_index("ctx")
    z = me // lanes
    lane = lax.rem(me, lanes)
    y = lane // 2
    c = lax.rem(lane, 2)
    side = z * lanes + (1 - y) * 2 + c
    twin = z * lanes + y * 2 + (1 - c)
    not_top = z < zs - 1
    not_bottom = z > 0
    up = jnp.minimum(me + lanes, n - lanes + lane)
    down = jnp.maximum(me - lanes, lane)
    target = (up, down, side, twin)

    barrier = pltpu.get_barrier_semaphore()

    def greet(who):
        pl.semaphore_signal(
            barrier, inc=1, device_id={"ctx": who}, device_id_type=pl.DeviceIdType.MESH
        )

    greet(side)
    greet(twin)
    pl.when(not_top)(lambda: greet(up))
    pl.when(not_bottom)(lambda: greet(down))
    pl.semaphore_wait(barrier, 2 + not_top.astype(jnp.int32) + not_bottom.astype(jnp.int32))

    def copy(block, kv, route, src=None):
        return pltpu.make_async_remote_copy(
            src_ref=buf.at[block, kv] if src is None else src,
            dst_ref=buf.at[block, kv],
            send_sem=send_sem.at[block, kv, route],
            recv_sem=recv_sem.at[block, kv],
            device_id={"ctx": target[route]},
            device_id_type=pl.DeviceIdType.MESH,
        )

    own = (k_ref, v_ref)
    for kv in range(2):
        pl.when(not_top)(lambda: copy(me, kv, UP, own[kv]).start())
        pl.when(not_bottom)(lambda: copy(me, kv, DOWN, own[kv]).start())
        copy(me, kv, SIDE, own[kv]).start()
        copy(me, kv, TWIN, own[kv]).start()
    buf[me, 0] = k_ref[...]
    buf[me, 1] = v_ref[...]

    def at(zz, yy, cc):
        return zz * lanes + yy * 2 + cc

    def from_line(zz, onward, keep):
        block = at(zz, y, c)
        for kv in range(2):
            copy(block, kv, onward).wait_recv()
            pl.when(keep)(lambda: copy(block, kv, onward).start())
            copy(block, kv, SIDE).start()
            copy(block, kv, TWIN).start()

    def from_side(zz):
        block = at(zz, 1 - y, c)
        for kv in range(2):
            copy(block, kv, TWIN).wait_recv()
            copy(block, kv, TWIN).start()

    def from_twin(zz):
        for yy in (y, 1 - y):
            for kv in range(2):
                copy(at(zz, yy, 1 - c), kv, TWIN).wait_recv()

    def both(s, low, high):
        pl.when(z >= s)(lambda: low(z - s))
        pl.when(z + s < zs)(lambda: high(z + s))

    for s in range(1, zs):
        both(s, lambda zz: from_line(zz, UP, not_top), lambda zz: from_line(zz, DOWN, not_bottom))
        if s == 1:
            from_side(z)
        else:
            both(s - 1, from_side, from_side)
    both(zs - 1, from_side, from_side)
    from_twin(z)
    for s in range(1, zs):
        both(s, from_twin, from_twin)

    for kv in range(2):
        pl.when(not_top)(lambda: copy(me, kv, UP, own[kv]).wait_send())
        pl.when(not_bottom)(lambda: copy(me, kv, DOWN, own[kv]).wait_send())
        copy(me, kv, SIDE, own[kv]).wait_send()
        copy(me, kv, TWIN, own[kv]).wait_send()

    def line_sent(zz, onward, keep):
        for kv in range(2):
            pl.when(keep)(lambda: copy(at(zz, y, c), kv, onward).wait_send())
            copy(at(zz, y, c), kv, SIDE).wait_send()
            copy(at(zz, y, c), kv, TWIN).wait_send()

    def side_sent(zz):
        for kv in range(2):
            copy(at(zz, 1 - y, c), kv, TWIN).wait_send()

    side_sent(z)
    for s in range(1, zs):
        both(s, lambda zz: line_sent(zz, UP, not_top), lambda zz: line_sent(zz, DOWN, not_bottom))
        both(s, side_sent, side_sent)


def attend_kernel(n, heads, span, q_ref, kv_ref, order_ref, out_ref, kl, vl, lim, top, acc):
    head_size = kl.shape[1]
    me = lax.axis_index("ctx")
    first = order_ref[2 * me]
    second = order_ref[2 * me + 1]
    p = jnp.minimum(first, second)
    low_at = (second < first).astype(jnp.int32)
    chunks_low = (p + 2) // 2
    base = 2 * chunks_low
    slots = 2 * (n + 1)

    def put(slot, block, half, limit):
        dst = pl.ds(pl.multiple_of(slot * span, span), span)
        src = pl.ds(pl.multiple_of(half * span, span), span)
        kl[dst, :] = kv_ref[block, 0, src, :]
        vl[dst, :] = kv_ref[block, 1, src, :]
        lim[slot] = limit

    put(base - 1, me, low_at, -span)
    put(slots - 1, me, low_at, -span)
    put(0, me, low_at, 0)
    put(base, me, 1 - low_at, 0)

    def place(d, carry):
        q = jnp.minimum(order_ref[2 * d], order_ref[2 * d + 1])
        lo = (order_ref[2 * d + 1] < order_ref[2 * d]).astype(jnp.int32)

        @pl.when(q < p)
        def _():
            put(q + 1, d, lo, span)

        @pl.when(q > p)
        def _():
            put(base + q - p, d, 1 - lo, span)

        put(base + n - p + d, d, lo, span)
        return carry

    lax.fori_loop(0, n, place, 0)

    top[...] = jnp.full_like(top, NEG)
    acc[...] = jnp.zeros_like(acc)
    factor = math.log2(math.e) / math.sqrt(head_size)
    ones = jnp.ones((2 * span, head_size), jnp.bfloat16)
    ahead = lax.broadcasted_iota(jnp.int32, (span, span), 1) - lax.broadcasted_iota(
        jnp.int32, (span, span), 0
    )

    def step(i, carry):
        high = (i >= chunks_low).astype(jnp.int32)
        half = jnp.where(high == 1, 1 - low_at, low_at)
        rows = pl.ds(pl.multiple_of(half * span, span), span)
        at = pl.ds(pl.multiple_of(i * 2 * span, 2 * span), 2 * span)
        keys = kl[at, :]
        vals = jnp.concatenate([vl[at, :], ones], axis=1)
        kept = jnp.concatenate([ahead <= lim[2 * i], ahead <= lim[2 * i + 1]], axis=1)
        for h in range(heads):
            q = q_ref[rows, h * head_size : (h + 1) * head_size]
            score = lax.dot_general(
                q, keys, (((1,), (1,)), ((), ())), preferred_element_type=jnp.float32
            )
            score = jnp.where(kept, score * factor, NEG)
            old = top[high, h]
            fresh = jnp.maximum(old, jnp.max(score, axis=1, keepdims=True))
            weight = jnp.exp2(score - jnp.concatenate([fresh, fresh], axis=1))
            fade = jnp.exp2(old - fresh)
            add = jnp.dot(
                weight.astype(jnp.bfloat16), vals, preferred_element_type=jnp.float32
            )
            acc[high, h] = acc[high, h] * jnp.concatenate([fade, fade], axis=1) + add
            top[high, h] = fresh
        return carry

    lax.fori_loop(0, n + 1, step, 0)

    for t in range(2):
        half = jnp.where(t == 1, 1 - low_at, low_at)
        rows = pl.ds(pl.multiple_of(half * span, span), span)
        for h in range(heads):
            out_ref[rows, h * head_size : (h + 1) * head_size] = (
                acc[t, h, :, :head_size] / acc[t, h, :, head_size:]
            ).astype(jnp.bfloat16)


def body(n, queries, keys, values, span_order):
    local_rows, width = queries.shape
    head_size = keys.shape[1]
    heads = width // head_size
    span = local_rows // 2
    vmem = pl.BlockSpec(memory_space=pltpu.VMEM)
    gathered = pl.pallas_call(
        functools.partial(gather_kernel, n),
        out_shape=jax.ShapeDtypeStruct((n, 2, local_rows, head_size), jnp.bfloat16),
        in_specs=[vmem, vmem],
        out_specs=vmem,
        scratch_shapes=[
            pltpu.SemaphoreType.DMA((n, 2, 4)),
            pltpu.SemaphoreType.DMA((n, 2)),
        ],
        compiler_params=pltpu.CompilerParams(collective_id=0, has_side_effects=True),
        name="gather",
    )(keys, values)
    slots = 2 * (n + 1)
    return pl.pallas_call(
        functools.partial(attend_kernel, n, heads, span),
        out_shape=jax.ShapeDtypeStruct((local_rows, width), jnp.bfloat16),
        in_specs=[vmem, vmem, pl.BlockSpec(memory_space=pltpu.SMEM)],
        out_specs=vmem,
        scratch_shapes=[
            pltpu.VMEM((slots * span, head_size), jnp.bfloat16),
            pltpu.VMEM((slots * span, head_size), jnp.bfloat16),
            pltpu.SMEM((slots,), jnp.int32),
            pltpu.VMEM((2, heads, span, head_size), jnp.float32),
            pltpu.VMEM((2, heads, span, 2 * head_size), jnp.float32),
        ],
        name="attend",
    )(queries, gathered, span_order)


def solution(mesh):
    in_specs = (
        P(("groups", "ctx"), None),
        P(("groups", "ctx"), None),
        P(("groups", "ctx"), None),
        P("groups"),
    )
    out_specs = P(("groups", "ctx"), None)
    return jax.shard_map(
        functools.partial(body, mesh.shape["ctx"]),
        mesh=mesh,
        in_specs=in_specs,
        out_specs=out_specs,
        check_vma=False,
    )
```

time: 142 us -> 38.9 us (0.27)
  waiting for transfers between devices: 79.9 us -> 0 us
  Pallas kernels: 0 us -> 38.7 us
  matrix products: 33.9 us -> 0 us
  between operations: 13.5 us -> 0.01 us
  other arithmetic: 11.2 us -> 0 us
  local copies, waits for them, and re-layouts: 2.23 us -> 0 us
    all_gather x2 -> x0, waiting for transfers between devices: 78.5 us -> none  [the longest x1 39.5 us: body(): key_piece = lax.all_gather(keys, 'ctx', axis=0, tiled=True)]
    pallas_call x0 -> x2, Pallas kernels: none -> 38.7 us  [the longest x1 24.3 us: body(): pl.pallas_call(functools.partial(gather_kernel, n), out_shape=jax.ShapeDt...]
    dot_general x16 -> x0, matrix products: 33.9 us -> none  [the longest x8 20.4 us: update(): jnp.einsum('hqk,kd->hqd', weight.astype(jnp.bfloat16), value_blk, preferr...]
    reduce_sum x8 -> x0, other arithmetic: 8.06 us -> none  [update(): total = total * factor + jnp.sum(weight, axis=-1)]
    unnamed x2 -> x0, local copies, waits for them, and re-layouts: 1.52 us -> none
  transfers between devices with their start and end apart: 2 -> 0, of which waited for: 2 -> 0; matrix products, arithmetic and copies ran while one was open for 2% -> 0% of each run, Pallas kernels for 0% -> 0%
where the time goes in v1:
time: 38.9 us; the launch traced here: 38.7 us
  Pallas kernels  38.7 us (99%)
    pallas_call x1, Pallas kernels, body(): pl.pallas_call(functools.partial(gather_kernel, n), out_shape=jax.ShapeDt...  24.3 us
    pallas_call x1, Pallas kernels, body(): pl.pallas_call(functools.partial(attend_kernel, n, heads, span), out_shap...  14.4 us

profile of v1, /device:TPU:1, one launch (start us, length us, event | category | flops | bytes accessed | tf_op | source)
XLA Modules:
  0.0 38.7 jit_solution(17977273184260620042)
XLA Ops:
  0.0 24.3 %gather.1.kv_ref = bf16[16,2,256,128]{3,2,1,0:T(8,128)(2,1)} custom-call(bf16[256,128]{1,0:T(8,128)(2,1)} %k_ref.1, bf16[256,128]{1,0:T(8,128)(2,1)} %v_ref.1), custom_call_target="tpu_custom_call" | custom-call | tf_op jit(solution)/shard_map/gather/pallas_call | solution.py:212
  24.3 14.4 %attend.1 = bf16[256,1024]{1,0:T(8,128)(2,1)} custom-call(bf16[256,1024]{1,0:T(8,128)(2,1)} %q_ref.1, bf16[16,2,256,128]{3,2,1,0:T(8,128)(2,1)} %gather.1.kv_ref, s32[32]{0:T(128)} %order_ref.1), custom_call_target="tpu_custom_call" | custom-call | tf_op jit(solution)/shard_map/attend/pallas_call | solution.py:225

commit v2 on v0

v2 whole, which is shorter than its diff:
```python
import functools
import math

import jax
import jax.numpy as jnp
from jax import lax
from jax.experimental import pallas as pl
from jax.experimental.pallas import tpu as pltpu
from jax.sharding import PartitionSpec as P

UP, DOWN, SIDE, TWIN = 0, 1, 2, 3
NEG = -1e30


def attend_kernel(
    n,
    heads,
    span,
    q_ref,
    k_ref,
    v_ref,
    order_ref,
    out_ref,
    buf,
    qs,
    k1,
    v1,
    k2,
    v2,
    top,
    part,
    acc,
    mix,
    send_sem,
    recv_sem,
):
    head_size = k1.shape[1]
    lanes = 4
    zs = n // lanes
    me = lax.axis_index("ctx")
    z = me // lanes
    lane = lax.rem(me, lanes)
    y = lane // 2
    c = lax.rem(lane, 2)
    side = z * lanes + (1 - y) * 2 + c
    twin = z * lanes + y * 2 + (1 - c)
    not_top = z < zs - 1
    not_bottom = z > 0
    up = jnp.minimum(me + lanes, n - lanes + lane)
    down = jnp.maximum(me - lanes, lane)

    barrier = pltpu.get_barrier_semaphore()

    def greet(who):
        pl.semaphore_signal(
            barrier, inc=1, device_id={"ctx": who}, device_id_type=pl.DeviceIdType.MESH
        )

    greet(side)
    greet(twin)
    pl.when(not_top)(lambda: greet(up))
    pl.when(not_bottom)(lambda: greet(down))
    pl.semaphore_wait(barrier, 2 + not_top.astype(jnp.int32) + not_bottom.astype(jnp.int32))

    def copy(block, kv, route, to, src=None):
        return pltpu.make_async_remote_copy(
            src_ref=buf.at[block, kv] if src is None else src,
            dst_ref=buf.at[block, kv],
            send_sem=send_sem.at[block, kv, route],
            recv_sem=recv_sem.at[block, kv],
            device_id={"ctx": to},
            device_id_type=pl.DeviceIdType.MESH,
        )

    own = (k_ref, v_ref)
    for kv in range(2):
        pl.when(not_top)(lambda: copy(me, kv, UP, up, own[kv]).start())
        pl.when(not_bottom)(lambda: copy(me, kv, DOWN, down, own[kv]).start())
        copy(me, kv, SIDE, side, own[kv]).start()
        copy(me, kv, TWIN, twin, own[kv]).start()

    def at(zz, yy, cc):
        return zz * lanes + yy * 2 + cc

    paired = jnp.minimum(z, zs - 1 - z)
    longer = jnp.where(z > zs - 1 - z, -1, 1)

    def level(r):
        near = jnp.where(lax.rem(r, 2) == 1, (r + 1) // 2, -((r + 1) // 2))
        return z + jnp.where(r <= 2 * paired, near, longer * (r - paired))

    def from_line(r):
        zz = level(r)
        block = at(zz, y, c)
        onward = jnp.where(zz < z, up, down)
        below = (zz < z).astype(jnp.int32)
        keep = below * not_top.astype(jnp.int32) + (1 - below) * not_bottom.astype(jnp.int32)
        for kv in range(2):
            copy(block, kv, UP, onward).wait_recv()
            pl.when(keep == 1)(lambda: copy(block, kv, UP, onward).start())
            copy(block, kv, SIDE, side).start()
            copy(block, kv, TWIN, twin).start()

    def from_side(r):
        block = at(level(r), 1 - y, c)
        for kv in range(2):
            copy(block, kv, TWIN, twin).wait_recv()
            copy(block, kv, TWIN, twin).start()

    factor = math.log2(math.e) / math.sqrt(head_size)
    first = order_ref[2 * me]
    second = order_ref[2 * me + 1]
    p = jnp.minimum(first, second)
    low_at = (second < first).astype(jnp.int32)
    ahead = lax.broadcasted_iota(jnp.int32, (span, span), 1) - lax.broadcasted_iota(
        jnp.int32, (span, span), 0
    )
    halves = (slice(0, span), slice(span, 2 * span))

    def facts(d):
        a = order_ref[2 * d]
        b = order_ref[2 * d + 1]
        return (b < a), jnp.minimum(a, b) < p

    def pick(flag, a, b):
        if isinstance(flag, bool):
            return a if flag else b
        return jnp.where(flag, a, b)

    def scores(q, keys):
        return (
            lax.dot_general(q, keys, (((1,), (1,)), ((), ())), preferred_element_type=jnp.float32)
            * factor
        )

    def wide(x):
        return jnp.concatenate([x, x], axis=1)

    def fill_first(slot, ks, vs, swapped):
        k1[halves[slot], :] = jnp.where(swapped, ks[1], ks[0])
        v1[halves[slot], :head_size] = jnp.where(swapped, vs[1], vs[0])

    def fill_second(slot, key, value, is_low):
        k2[halves[slot], :] = key
        zero = jnp.zeros_like(value)
        v2[halves[slot], :head_size] = pick(is_low, value, zero)
        v2[halves[slot], head_size:] = pick(is_low, zero, value)

    def pieces(d, is_own=False):
        if is_own:
            return [k_ref[s, :] for s in halves], [v_ref[s, :] for s in halves]
        return [buf[d, 0, s, :] for s in halves], [buf[d, 1, s, :] for s in halves]

    def high_update(h):
        score = scores(qs[1, h], k1[...])
        old = top[0, h]
        fresh = jnp.maximum(old, jnp.max(score, axis=1, keepdims=True))
        weight = jnp.exp2(score - wide(fresh)).astype(jnp.bfloat16)
        fade = jnp.exp2(old - fresh)
        add = jnp.dot(weight, v1[...], preferred_element_type=jnp.float32)
        acc[h] = acc[h] * wide(fade) + add
        top[0, h] = fresh

    def mixed_update(h, lows, diagonal=False):
        old_low, old_high = top[1, h], top[2, h]
        fresh_low, fresh_high = old_low, old_high
        made = []
        for j, is_low in enumerate(lows):
            score = scores(pick(is_low, qs[0, h], qs[1, h]), k2[halves[j], :])
            if diagonal:
                score = jnp.where(ahead <= 0, score, NEG)
            most = jnp.broadcast_to(jnp.max(score, axis=1, keepdims=True), score.shape)
            fresh_low = pick(is_low, jnp.maximum(fresh_low, most), fresh_low)
            fresh_high = pick(is_low, fresh_high, jnp.maximum(fresh_high, most))
            made.append(score)
        fade_low = jnp.exp2(old_low - fresh_low)
        fade_high = jnp.exp2(old_high - fresh_high)
        part_low = part[0, h] * fade_low
        part_high = part[1, h] * fade_high
        weights = []
        for score, is_low in zip(made, lows):
            weight = jnp.exp2(score - pick(is_low, fresh_low, fresh_high))
            part_low = pick(is_low, part_low + weight, part_low)
            part_high = pick(is_low, part_high, part_high + weight)
            weights.append(weight.astype(jnp.bfloat16))
        size = len(lows) * span
        add = jnp.dot(
            jnp.concatenate(weights, axis=1), v2[:size, :], preferred_element_type=jnp.float32
        )
        mix[h] = mix[h] * jnp.concatenate([fade_low, fade_high], axis=1) + add
        top[1, h] = fresh_low
        top[2, h] = fresh_high
        part[0, h] = part_low
        part[1, h] = part_high

    top[...] = jnp.full_like(top, NEG)
    part[...] = jnp.zeros_like(part)
    acc[...] = jnp.zeros_like(acc)
    mix[...] = jnp.zeros_like(mix)
    v1[:, head_size:] = jnp.ones_like(v1[:, head_size:])

    ks, vs = pieces(me, True)
    swapped = low_at == 1
    for h in range(heads):
        cols = slice(h * head_size, (h + 1) * head_size)
        rows = [q_ref[s, cols] for s in halves]
        qs[0, h] = jnp.where(swapped, rows[1], rows[0])
        qs[1, h] = jnp.where(swapped, rows[0], rows[1])
    fill_first(0, ks, vs, swapped)
    fill_second(0, jnp.where(swapped, ks[1], ks[0]), jnp.where(swapped, vs[1], vs[0]), True)
    fill_second(1, jnp.where(swapped, ks[0], ks[1]), jnp.where(swapped, vs[0], vs[1]), False)
    for h in range(heads):
        mixed_update(h, (True, False), diagonal=True)

    def fill_remote(d, slot1, slot2):
        ks, vs = pieces(d)
        swapped, is_low = facts(d)
        fill_first(slot1, ks, vs, swapped)
        other = jnp.logical_xor(swapped, jnp.logical_not(is_low))
        fill_second(
            slot2, jnp.where(other, ks[1], ks[0]), jnp.where(other, vs[1], vs[0]), is_low
        )
        return is_low

    def arrived(d):
        for kv in range(2):
            copy(d, kv, TWIN, twin).wait_recv()

    arrived(twin)
    is_low = fill_remote(twin, 1, 0)
    for h in range(heads):
        high_update(h)
        mixed_update(h, (is_low,))
    from_line(jnp.int32(1))

    last = 2 * zs - 2

    def step(t, carry):
        ends = (t == last).astype(jnp.int32)
        sideways = jnp.maximum(lax.rem(t, 2), ends)
        k = jnp.where(ends == 1, zs - 1, t // 2)

        @pl.when(sideways == 1)
        def _():
            from_side(k)

        @pl.when((1 - sideways) * (k + 2 < zs).astype(jnp.int32) == 1)
        def _():
            from_line(k + 2)

        zz = level(jnp.where(sideways == 1, k, k + 1))
        yy = jnp.where(sideways == 1, 1 - y, y)
        near = at(zz, yy, c)
        far = at(zz, yy, 1 - c)
        arrived(far)
        lows = (fill_remote(near, 0, 0), fill_remote(far, 1, 1))
        for h in range(heads):
            high_update(h)
            mixed_update(h, lows)
        return carry

    lax.fori_loop(0, last + 1, step, 0)

    for h in range(heads):
        cols = slice(h * head_size, (h + 1) * head_size)
        sum_low = jnp.sum(part[0, h], axis=1, keepdims=True)
        sum_high = jnp.sum(part[1, h], axis=1, keepdims=True)
        most = jnp.maximum(top[0, h], top[2, h])
        fade1 = jnp.exp2(top[0, h] - most)
        fade2 = jnp.exp2(top[2, h] - most)
        low = mix[h, :, :head_size] / sum_low
        high = (acc[h, :, :head_size] * fade1 + mix[h, :, head_size:] * fade2) / (
            acc[h, :, head_size:] * fade1 + sum_high * fade2
        )
        out_ref[halves[0], cols] = jnp.where(swapped, high, low).astype(jnp.bfloat16)
        out_ref[halves[1], cols] = jnp.where(swapped, low, high).astype(jnp.bfloat16)

    for kv in range(2):
        pl.when(not_top)(lambda: copy(me, kv, UP, up, own[kv]).wait_send())
        pl.when(not_bottom)(lambda: copy(me, kv, DOWN, down, own[kv]).wait_send())
        copy(me, kv, SIDE, side, own[kv]).wait_send()
        copy(me, kv, TWIN, twin, own[kv]).wait_send()

    def line_sent(r, carry):
        zz = level(r)
        block = at(zz, y, c)
        onward = jnp.where(zz < z, up, down)
        below = (zz < z).astype(jnp.int32)
        keep = below * not_top.astype(jnp.int32) + (1 - below) * not_bottom.astype(jnp.int32)
        for kv in range(2):
            pl.when(keep == 1)(lambda: copy(block, kv, UP, onward).wait_send())
            copy(block, kv, SIDE, side).wait_send()
            copy(block, kv, TWIN, twin).wait_send()
        return carry

    lax.fori_loop(1, zs, line_sent, 0)

    def side_sent(r, carry):
        for kv in range(2):
            copy(at(r, 1 - y, c), kv, TWIN, twin).wait_send()
        return carry

    lax.fori_loop(0, zs, side_sent, 0)


def body(n, queries, keys, values, span_order):
    local_rows, width = queries.shape
    head_size = keys.shape[1]
    heads = width // head_size
    span = local_rows // 2
    vmem = pl.BlockSpec(memory_space=pltpu.VMEM)
    return pl.pallas_call(
        functools.partial(attend_kernel, n, heads, span),
        out_shape=jax.ShapeDtypeStruct((local_rows, width), jnp.bfloat16),
        in_specs=[vmem, vmem, vmem, pl.BlockSpec(memory_space=pltpu.SMEM)],
        out_specs=vmem,
        scratch_shapes=[
            pltpu.VMEM((n, 2, local_rows, head_size), jnp.bfloat16),
            pltpu.VMEM((2, heads, span, head_size), jnp.bfloat16),
            pltpu.VMEM((local_rows, head_size), jnp.bfloat16),
            pltpu.VMEM((local_rows, 2 * head_size), jnp.bfloat16),
            pltpu.VMEM((local_rows, head_size), jnp.bfloat16),
            pltpu.VMEM((local_rows, 2 * head_size), jnp.bfloat16),
            pltpu.VMEM((3, heads, span, head_size), jnp.float32),
            pltpu.VMEM((2, heads, span, head_size), jnp.float32),
            pltpu.VMEM((heads, span, 2 * head_size), jnp.float32),
            pltpu.VMEM((heads, span, 2 * head_size), jnp.float32),
            pltpu.SemaphoreType.DMA((n, 2, 4)),
            pltpu.SemaphoreType.DMA((n, 2)),
        ],
        compiler_params=pltpu.CompilerParams(collective_id=0, has_side_effects=True),
        name="attend",
    )(queries, keys, values, span_order)


def solution(mesh):
    in_specs = (
        P(("groups", "ctx"), None),
        P(("groups", "ctx"), None),
        P(("groups", "ctx"), None),
        P("groups"),
    )
    out_specs = P(("groups", "ctx"), None)
    return jax.shard_map(
        functools.partial(body, mesh.shape["ctx"]),
        mesh=mesh,
        in_specs=in_specs,
        out_specs=out_specs,
        check_vma=False,
    )
```

time: 142 us -> 43.3 us (0.30)
  waiting for transfers between devices: 79.9 us -> 0 us
  Pallas kernels: 0 us -> 41.3 us
  matrix products: 33.9 us -> 0 us
  between operations: 13.5 us -> 0.01 us
  other arithmetic: 11.2 us -> 0 us
    all_gather x2 -> x0, waiting for transfers between devices: 78.5 us -> none  [the longest x1 39.5 us: body(): key_piece = lax.all_gather(keys, 'ctx', axis=0, tiled=True)]
    pallas_call x0 -> x1, Pallas kernels: none -> 41.3 us  [body(): pl.pallas_call(functools.partial(attend_kernel, n, heads, span), out_shap...]
    dot_general x16 -> x0, matrix products: 33.9 us -> none  [the longest x8 20.4 us: update(): jnp.einsum('hqk,kd->hqd', weight.astype(jnp.bfloat16), value_blk, preferr...]
    reduce_sum x8 -> x0, other arithmetic: 8.06 us -> none  [update(): total = total * factor + jnp.sum(weight, axis=-1)]
  transfers between devices with their start and end apart: 2 -> 0, of which waited for: 2 -> 0; matrix products, arithmetic and copies ran while one was open for 2% -> 0% of each run, Pallas kernels for 0% -> 0%
where the time goes in v2:
time: 43.3 us; the launch traced here: 43.2 us
  Pallas kernels  41.3 us (95%)
  local copies, waits for them, and re-layouts  1.87 us (4%)
    pallas_call x1, Pallas kernels, body(): pl.pallas_call(functools.partial(attend_kernel, n, heads, span), out_shap...  41.3 us
    unnamed x1, local copies, waits for them, and re-layouts  1.87 us

profile of v2, /device:TPU:1, one launch (start us, length us, event | category | flops | bytes accessed | tf_op | source)
XLA Modules:
  0.0 43.2 jit_solution(11256429060434770550)
XLA Ops:
  0.0 41.3 %attend.1 = bf16[256,1024]{1,0:T(8,128)(2,1)} custom-call(bf16[256,1024]{1,0:T(8,128)(2,1)} %q_ref.1, bf16[256,128]{1,0:T(8,128)(2,1)} %k_ref.1, bf16[256,128]{1,0:T(8,128)(2,1)} %v_ref.1, s32[32]{0:T(128)} %order_ref.1), custom_call_target="tpu_custom_call" | custom-call | tf_op jit(solution)/shard_map/attend/pallas_call | solution.py:312
  41.3 1.9 %copy.6 = bf16[256,1024]{1,0:T(8,128)(2,1)} copy(bf16[256,1024]{1,0:T(8,128)(2,1)} %attend.1) | data formatting | bytes 1048576

commit v3 on v1

--- a/solution.py
+++ b/solution.py
@@ -119,88 +119,132 @@
         both(s, side_sent, side_sent)
 
 
-def attend_kernel(n, heads, span, q_ref, kv_ref, order_ref, out_ref, kl, vl, lim, top, acc):
-    head_size = kl.shape[1]
+def attend_kernel(
+    n, heads, span, q_ref, kv_ref, order_ref, out_ref, qs, k1, v1, k2, v2, raw1, raw2, w1, w2
+):
+    head_size = k1.shape[1]
     me = lax.axis_index("ctx")
     first = order_ref[2 * me]
     second = order_ref[2 * me + 1]
     p = jnp.minimum(first, second)
-    low_at = (second < first).astype(jnp.int32)
-    chunks_low = (p + 2) // 2
-    base = 2 * chunks_low
-    slots = 2 * (n + 1)
-
-    def put(slot, block, half, limit):
-        dst = pl.ds(pl.multiple_of(slot * span, span), span)
-        src = pl.ds(pl.multiple_of(half * span, span), span)
-        kl[dst, :] = kv_ref[block, 0, src, :]
-        vl[dst, :] = kv_ref[block, 1, src, :]
-        lim[slot] = limit
-
-    put(base - 1, me, low_at, -span)
-    put(slots - 1, me, low_at, -span)
-    put(0, me, low_at, 0)
-    put(base, me, 1 - low_at, 0)
+    swapped = second < first
+    low_at = swapped.astype(jnp.int32)
+    pad_high = lax.rem(p, 2)
+    pad_low = 1 - pad_high
+    chunks_low = (p + 1 + pad_low) // 2
+    halves = (slice(0, span), slice(span, 2 * span))
+
+    def rows_of(slot):
+        return pl.ds(pl.multiple_of(slot * span, span), span)
+
+    def put(slot, block, half, is_low):
+        k2[rows_of(slot), :] = kv_ref[block, 0, rows_of(half), :]
+        value = kv_ref[block, 1, rows_of(half), :]
+        zero = jnp.zeros_like(value)
+        v2[rows_of(slot), :head_size] = jnp.where(is_low, value, zero)
+        v2[rows_of(slot), head_size:] = jnp.where(is_low, zero, value)
+
+    put(1, me, low_at, True)
+    put(n, me, low_at, False)
+    put(0, me, low_at, True)
+    put(n + 1, me, 1 - low_at, False)
 
     def place(d, carry):
         q = jnp.minimum(order_ref[2 * d], order_ref[2 * d + 1])
         lo = (order_ref[2 * d + 1] < order_ref[2 * d]).astype(jnp.int32)
-
-        @pl.when(q < p)
+        is_low = q < p
+
+        @pl.when(q != p)
         def _():
-            put(q + 1, d, lo, span)
-
-        @pl.when(q > p)
-        def _():
-            put(base + q - p, d, 1 - lo, span)
-
-        put(base + n - p + d, d, lo, span)
+            slot = jnp.where(is_low, q + 1 + pad_low, n + 1 - pad_high - (q - p))
+            put(slot, d, jnp.where(is_low, lo, 1 - lo), is_low)
+
+        k1[rows_of(d), :] = kv_ref[d, 0, rows_of(lo), :]
+        v1[rows_of(d), :head_size] = kv_ref[d, 1, rows_of(lo), :]
         return carry
 
     lax.fori_loop(0, n, place, 0)
-
-    top[...] = jnp.full_like(top, NEG)
-    acc[...] = jnp.zeros_like(acc)
+    v1[:, head_size:] = jnp.ones_like(v1[:, head_size:])
+    for h in range(heads):
+        cols = slice(h * head_size, (h + 1) * head_size)
+        pair = [q_ref[s, cols] for s in halves]
+        qs[0, h] = jnp.where(swapped, pair[1], pair[0])
+        qs[1, h] = jnp.where(swapped, pair[0], pair[1])
+
     factor = math.log2(math.e) / math.sqrt(head_size)
-    ones = jnp.ones((2 * span, head_size), jnp.bfloat16)
     ahead = lax.broadcasted_iota(jnp.int32, (span, span), 1) - lax.broadcasted_iota(
         jnp.int32, (span, span), 0
     )
-
-    def step(i, carry):
-        high = (i >= chunks_low).astype(jnp.int32)
-        half = jnp.where(high == 1, 1 - low_at, low_at)
-        rows = pl.ds(pl.multiple_of(half * span, span), span)
-        at = pl.ds(pl.multiple_of(i * 2 * span, 2 * span), 2 * span)
-        keys = kl[at, :]
-        vals = jnp.concatenate([vl[at, :], ones], axis=1)
-        kept = jnp.concatenate([ahead <= lim[2 * i], ahead <= lim[2 * i + 1]], axis=1)
-        for h in range(heads):
-            q = q_ref[rows, h * head_size : (h + 1) * head_size]
-            score = lax.dot_general(
-                q, keys, (((1,), (1,)), ((), ())), preferred_element_type=jnp.float32
-            )
-            score = jnp.where(kept, score * factor, NEG)
-            old = top[high, h]
-            fresh = jnp.maximum(old, jnp.max(score, axis=1, keepdims=True))
-            weight = jnp.exp2(score - jnp.concatenate([fresh, fresh], axis=1))
-            fade = jnp.exp2(old - fresh)
-            add = jnp.dot(
-                weight.astype(jnp.bfloat16), vals, preferred_element_type=jnp.float32
-            )
-            acc[high, h] = acc[high, h] * jnp.concatenate([fade, fade], axis=1) + add
-            top[high, h] = fresh
+    kept_first = jnp.concatenate([ahead <= 0, ahead <= span - 2 * span * pad_low], axis=1)
+    kept_last = jnp.concatenate([ahead <= span - 2 * span * pad_high, ahead <= 0], axis=1)
+    chunks1 = n // 2
+    chunks2 = n // 2 + 1
+    wide = 2 * span
+
+    def scores(q, keys):
+        return (
+            lax.dot_general(q, keys, (((1,), (1,)), ((), ())), preferred_element_type=jnp.float32)
+            * factor
+        )
+
+    def folded(x, op):
+        return op(x[:, :span], x[:, span:])
+
+    def one_head(h, b):
+        high = jnp.full((span, span), NEG, jnp.float32)
+        low = high
+        for i in range(chunks1):
+            cols = slice(i * wide, (i + 1) * wide)
+            score = scores(qs[1, h], k1[cols, :])
+            raw1[b, :, cols] = score
+            high = jnp.maximum(high, folded(score, jnp.maximum))
+        for i in range(chunks2):
+            cols = slice(i * wide, (i + 1) * wide)
+            is_low = i < chunks_low
+            score = scores(qs[1 - is_low.astype(jnp.int32), h], k2[cols, :])
+            if i == 0:
+                score = jnp.where(kept_first, score, NEG)
+            if i == chunks2 - 1:
+                score = jnp.where(kept_last, score, NEG)
+            raw2[b, :, cols] = score
+            most = folded(score, jnp.maximum)
+            low = jnp.where(is_low, jnp.maximum(low, most), low)
+            high = jnp.where(is_low, high, jnp.maximum(high, most))
+        low = jnp.broadcast_to(jnp.max(low, axis=1, keepdims=True), (span, span))
+        high = jnp.broadcast_to(jnp.max(high, axis=1, keepdims=True), (span, span))
+        for i in range(chunks1):
+            cols = slice(i * wide, (i + 1) * wide)
+            shift = jnp.concatenate([high, high], axis=1)
+            w1[b, :, cols] = jnp.exp2(raw1[b, :, cols] - shift).astype(jnp.bfloat16)
+        sum_low = jnp.zeros((span, span), jnp.float32)
+        sum_high = sum_low
+        for i in range(chunks2):
+            cols = slice(i * wide, (i + 1) * wide)
+            is_low = i < chunks_low
+            shift = jnp.where(is_low, low, high)
+            weight = jnp.exp2(raw2[b, :, cols] - jnp.concatenate([shift, shift], axis=1))
+            w2[b, :, cols] = weight.astype(jnp.bfloat16)
+            add = folded(weight, jnp.add)
+            sum_low = jnp.where(is_low, sum_low + add, sum_low)
+            sum_high = jnp.where(is_low, sum_high, sum_high + add)
+        got1 = jnp.dot(w1[b], v1[...], preferred_element_type=jnp.float32)
+        got2 = jnp.dot(w2[b], v2[...], preferred_element_type=jnp.float32)
+        sum_low = jnp.sum(sum_low, axis=1, keepdims=True)
+        sum_high = jnp.sum(sum_high, axis=1, keepdims=True)
+        out_low = got2[:, :head_size] / sum_low
+        out_high = (got1[:, :head_size] + got2[:, head_size:]) / (got1[:, head_size:] + sum_high)
+        cols = pl.ds(pl.multiple_of(h * head_size, head_size), head_size)
+        out_ref[halves[0], cols] = jnp.where(swapped, out_high, out_low).astype(jnp.bfloat16)
+        out_ref[halves[1], cols] = jnp.where(swapped, out_low, out_high).astype(jnp.bfloat16)
+
+    together = 2 if chunks1 <= heads else 1
+
+    def some_heads(g, carry):
+        for b in range(together):
+            one_head(g * together + b, b)
         return carry
 
-    lax.fori_loop(0, n + 1, step, 0)
-
-    for t in range(2):
-        half = jnp.where(t == 1, 1 - low_at, low_at)
-        rows = pl.ds(pl.multiple_of(half * span, span), span)
-        for h in range(heads):
-            out_ref[rows, h * head_size : (h + 1) * head_size] = (
-                acc[t, h, :, :head_size] / acc[t, h, :, head_size:]
-            ).astype(jnp.bfloat16)
+    lax.fori_loop(0, heads // together, some_heads, 0)
 
 
 def body(n, queries, keys, values, span_order):
@@ -221,18 +265,23 @@
         compiler_params=pltpu.CompilerParams(collective_id=0, has_side_effects=True),
         name="gather",
     )(keys, values)
-    slots = 2 * (n + 1)
+    half_keys = n * span
+    more_keys = (n + 2) * span
     return pl.pallas_call(
         functools.partial(attend_kernel, n, heads, span),
         out_shape=jax.ShapeDtypeStruct((local_rows, width), jnp.bfloat16),
         in_specs=[vmem, vmem, pl.BlockSpec(memory_space=pltpu.SMEM)],
         out_specs=vmem,
         scratch_shapes=[
-            pltpu.VMEM((slots * span, head_size), jnp.bfloat16),
-            pltpu.VMEM((slots * span, head_size), jnp.bfloat16),
-            pltpu.SMEM((slots,), jnp.int32),
-            pltpu.VMEM((2, heads, span, head_size), jnp.float32),
-            pltpu.VMEM((2, heads, span, 2 * head_size), jnp.float32),
+            pltpu.VMEM((2, heads, span, head_size), jnp.bfloat16),
+            pltpu.VMEM((half_keys, head_size), jnp.bfloat16),
+            pltpu.VMEM((half_keys, 2 * head_size), jnp.bfloat16),
+            pltpu.VMEM((more_keys, head_size), jnp.bfloat16),
+            pltpu.VMEM((more_keys, 2 * head_size), jnp.bfloat16),
+            pltpu.VMEM((2, span, half_keys), jnp.float32),
+            pltpu.VMEM((2, span, more_keys), jnp.float32),
+            pltpu.VMEM((2, span, half_keys), jnp.bfloat16),
+            pltpu.VMEM((2, span, more_keys), jnp.bfloat16),
         ],
         name="attend",
     )(queries, gathered, span_order)

time: 38.9 us -> 36.7 us (0.943)
  Pallas kernels: 38.7 us -> 36.4 us
    pallas_call x1, Pallas kernels: 14.4 us -> 12.1 us  [body(): pl.pallas_call(functools.partial(attend_kernel, n, heads, span), out_shap...]
where the time goes in v3:
time: 36.7 us; the launch traced here: 36.4 us
  Pallas kernels  36.4 us (99%)
    pallas_call x1, Pallas kernels, body(): pl.pallas_call(functools.partial(gather_kernel, n), out_shape=jax.ShapeDt...  24.3 us
    pallas_call x1, Pallas kernels, body(): pl.pallas_call(functools.partial(attend_kernel, n, heads, span), out_shap...  12.1 us

profile of v3, /device:TPU:1, one launch (start us, length us, event | category | flops | bytes accessed | tf_op | source)
XLA Modules:
  0.0 36.4 jit_solution(12180387991114226346)
XLA Ops:
  0.0 24.3 %gather.1.kv_ref = bf16[16,2,256,128]{3,2,1,0:T(8,128)(2,1)} custom-call(bf16[256,128]{1,0:T(8,128)(2,1)} %k_ref.1, bf16[256,128]{1,0:T(8,128)(2,1)} %v_ref.1), custom_call_target="tpu_custom_call" | custom-call | tf_op jit(solution)/shard_map/gather/pallas_call | solution.py:256
  24.3 12.1 %attend.1 = bf16[256,1024]{1,0:T(8,128)(2,1)} custom-call(bf16[256,1024]{1,0:T(8,128)(2,1)} %q_ref.1, bf16[16,2,256,128]{3,2,1,0:T(8,128)(2,1)} %gather.1.kv_ref, s32[32]{0:T(128)} %order_ref.1), custom_call_target="tpu_custom_call" | custom-call | tf_op jit(solution)/shard_map/attend/pallas_call | solution.py:270
